TPU v7x, 32 devices: a whole 2x2x4 slice. The times are simulated.
32 devices in a mesh: dp: 8 (over z, y), rep: 4 (over x, core).
Axes of the slice: x: 2, y: 2, z: 4, core: 2. Of those that a mesh axis runs over, the one named last changes fastest.
Arguments:
- enc: bfloat16 [64, 48, 640], P(('dp', 'rep')), may hold values from -6 to 6
- pred: bfloat16 [64, 17, 640], P(('dp', 'rep')), may hold values from -6 to 6
- labels: int32 [64, 16], P(('dp', 'rep')), may hold values from 1 to 4095
- frame_len: int32 [64], P(('dp', 'rep')), may hold values from 24 to 48, as said below
- label_len: int32 [64], P(('dp', 'rep')), may hold values from 1 to 16, as said below
- w_enc: bfloat16 [640, 640], replicated, may hold values from -0.25 to 0.25
- w_pred: bfloat16 [640, 640], replicated, may hold values from -0.25 to 0.25
- b_joint: bfloat16 [640], replicated, may hold values from -3 to 3
- w_out: bfloat16 [640, 4096], replicated, may hold values from -0.69921875 to 0.69921875
- b_out: bfloat16 [4096], replicated, may hold values from -5 to 5
Outputs:
- step_enc: float32 [640, 640], replicated
- step_pred: float32 [640, 640], replicated
- step_out: float32 [640, 4096], replicated
- step_bias_out: float32 [4096], replicated
- step_bias_joint: float32 [640], replicated
- mean_loss: float32 [], replicated
Inputs may be any that keep to these rules, and one draw needn't show every extreme that they name: `frame_len`: the last utterance has all 48 frames. `label_len`: the last utterance has all 16 labels.
All inputs are finite; a program needn't handle non-finite values.
Results may differ from a plain program's by a relative error of at most 0.0055.
Values sent between devices are 32-bit elements; how exact they have to be, the bound alone decides.
No kernel may reach another device: no remote copies, remote signals or barrier semaphores. Data moves between devices by JAX's collectives and lax.ppermute only.
A program may use at most 256 MiB of HBM per device.

v0:
```python
import jax
import jax.numpy as jnp
from jax import lax
from jax.sharding import PartitionSpec as P

NEG = -1e30
EPS = 1e-06


def diagonal_index(num_frames, count_labels):
    diagonals = jnp.arange(num_frames + count_labels - 1, dtype=jnp.int32)
    positions = jnp.arange(count_labels, dtype=jnp.int32)
    return diagonals[:, None] - positions[None, :]


def skewed(grid):
    utterances, num_frames, count_labels = grid.shape
    positions = jnp.arange(count_labels, dtype=jnp.int32)
    frame_index = diagonal_index(num_frames, count_labels)
    inside = (frame_index >= 0) & (frame_index < num_frames)
    picked = grid[:, jnp.clip(frame_index, 0, num_frames - 1), positions[None, :]]
    picked = jnp.where(inside[None, :, :], picked, NEG)
    return jnp.transpose(picked, (1, 0, 2))


def unskewed(diag_grid, num_frames):
    count_labels = diag_grid.shape[2]
    by_utterance = jnp.transpose(diag_grid, (1, 0, 2))
    frame_ids = jnp.arange(num_frames, dtype=jnp.int32)
    positions = jnp.arange(count_labels, dtype=jnp.int32)
    return by_utterance[:, frame_ids[:, None] + positions[None, :], positions[None, :]]


def lattice(blank, emit, frame_len, label_len):
    utterances, num_frames, count_labels = blank.shape
    positions = jnp.arange(count_labels, dtype=jnp.int32)
    frame_index = diagonal_index(num_frames, count_labels)
    blank_diag = skewed(blank)
    emit_diag = skewed(emit)
    neg_block = jnp.full((1, utterances, count_labels), NEG, jnp.float32)
    neg_col = jnp.full((utterances, 1), NEG, jnp.float32)
    neg_grid = jnp.full((utterances, count_labels), NEG, jnp.float32)
    frame_count = frame_len[:, None]
    label_count = label_len[:, None]
    terminal = jnp.where(positions[None, :] == label_count, 0.0, NEG).astype(jnp.float32)
    first_diag = jnp.broadcast_to(
        jnp.where(positions == 0, 0.0, NEG).astype(jnp.float32)[None, :], (utterances, count_labels)
    )
    blank_prev = jnp.concatenate([neg_block, blank_diag[:-1]], axis=0)
    emit_prev = jnp.concatenate([neg_block, emit_diag[:-1]], axis=0)
    steps_total = frame_index.shape[0]
    step_ids = jnp.arange(steps_total, dtype=jnp.int32)

    def both_ways(carry, inputs):
        alpha_prev, beta_next = carry
        step_id, blank_fwd, emit_fwd, frames_fwd, blank_back, emit_back, frames_back = inputs
        top_term = alpha_prev + blank_fwd
        left_term = jnp.concatenate([neg_col, (alpha_prev + emit_fwd)[:, :-1]], axis=1)
        alpha_cell = jnp.logaddexp(top_term, left_term)
        inside = (frames_fwd >= 0) & (frames_fwd < num_frames)
        alpha_cell = jnp.where(inside[None, :], alpha_cell, NEG)
        alpha_cell = jnp.where(step_id == 0, first_diag, alpha_cell)
        frames_row = frames_back[None, :]
        below = jnp.where(
            frames_row == frame_count - 1,
            terminal,
            jnp.where(frames_row >= frame_count, neg_grid, beta_next),
        )
        right_term = jnp.concatenate([beta_next[:, 1:], neg_col], axis=1)
        beta_cell = jnp.logaddexp(below + blank_back, right_term + emit_back)
        live = (positions[None, :] <= label_count) & (frames_row < frame_count) & (frames_row >= 0)
        beta_cell = jnp.where(live, beta_cell, NEG)
        return ((alpha_cell, beta_cell), (alpha_cell, beta_cell, below))

    inputs = (
        step_ids,
        blank_prev,
        emit_prev,
        frame_index,
        jnp.flip(blank_diag, 0),
        jnp.flip(emit_diag, 0),
        jnp.flip(frame_index, 0),
    )
    unused_last, (alpha_diag, beta_rev, below_rev) = lax.scan(
        both_ways, (first_diag, neg_grid), inputs
    )
    alpha = unskewed(alpha_diag, num_frames)
    beta = unskewed(jnp.flip(beta_rev, 0), num_frames)
    below = unskewed(jnp.flip(below_rev, 0), num_frames)
    return (alpha, beta, below)


def joint_forward(enc_row, pred_row, label_row, w_enc, w_pred, b_joint, w_out, b_out):
    num_frames = enc_row.shape[0]
    count_labels = pred_row.shape[0]
    joint_width = w_enc.shape[1]
    vocab_size = w_out.shape[1]
    enc_proj = jnp.dot(enc_row, w_enc, preferred_element_type=jnp.float32)
    pred_proj = jnp.dot(pred_row, w_pred, preferred_element_type=jnp.float32) + b_joint.astype(
        jnp.float32
    )
    hidden = jnp.tanh(enc_proj[:, None, :] + pred_proj[None, :, :]).astype(jnp.bfloat16)
    hidden = lax.optimization_barrier(hidden.reshape(num_frames * count_labels, joint_width))
    logits = jnp.dot(hidden, w_out, preferred_element_type=jnp.float32) + b_out.astype(jnp.float32)
    log_probs = jax.nn.log_softmax(logits, axis=-1)
    targets = jnp.concatenate([label_row, jnp.ones((1,), jnp.int32)])
    target_cols = jnp.tile(targets, num_frames)
    vocab_pos = jnp.arange(vocab_size, dtype=jnp.int32)
    is_target = vocab_pos[None, :] == target_cols[:, None]
    emit = jnp.sum(jnp.where(is_target, log_probs, 0.0), axis=1).reshape(num_frames, count_labels)
    blank = log_probs[:, 0].reshape(num_frames, count_labels)
    return (hidden, log_probs, blank, emit)


def joint_backward(
    enc_row, pred_row, label_row, hidden, log_probs, blank, emit, alpha, beta, below, w_out
):
    num_frames = enc_row.shape[0]
    count_labels = pred_row.shape[0]
    joint_width = hidden.shape[1]
    vocab_size = w_out.shape[1]
    targets = jnp.concatenate([label_row, jnp.ones((1,), jnp.int32)])
    target_cols = jnp.tile(targets, num_frames)
    vocab_pos = jnp.arange(vocab_size, dtype=jnp.int32)
    is_target = vocab_pos[None, :] == target_cols[:, None]
    log_total = beta[0, 0]
    right = jnp.concatenate([beta[:, 1:], jnp.full((num_frames, 1), NEG, jnp.float32)], axis=1)
    blank_occ = jnp.exp(alpha + blank + below - log_total).reshape(-1)
    emit_occ = jnp.exp(alpha + emit + right - log_total).reshape(-1)
    probs = jnp.exp(log_probs)
    grad_logits = probs * (blank_occ + emit_occ)[:, None]
    grad_logits = grad_logits - jnp.where(vocab_pos[None, :] == 0, blank_occ[:, None], 0.0)
    grad_logits = grad_logits - jnp.where(is_target, emit_occ[:, None], 0.0)
    grad_logits = lax.optimization_barrier(grad_logits.astype(jnp.bfloat16))
    grad_out = lax.dot_general(
        hidden, grad_logits, (((0,), (0,)), ((), ())), preferred_element_type=jnp.float32
    )
    grad_bias_out = jnp.sum(grad_logits.astype(jnp.float32), axis=0)
    grad_hidden = lax.dot_general(
        grad_logits, w_out, (((1,), (1,)), ((), ())), preferred_element_type=jnp.float32
    )
    hidden_wide = hidden.astype(jnp.float32)
    grad_pre = (grad_hidden * (1.0 - hidden_wide * hidden_wide)).reshape(
        num_frames, count_labels, joint_width
    )
    grad_enc_proj = lax.optimization_barrier(jnp.sum(grad_pre, axis=1).astype(jnp.bfloat16))
    grad_pred_proj = lax.optimization_barrier(jnp.sum(grad_pre, axis=0).astype(jnp.bfloat16))
    grad_enc = lax.dot_general(
        enc_row, grad_enc_proj, (((0,), (0,)), ((), ())), preferred_element_type=jnp.float32
    )
    grad_pred = lax.dot_general(
        pred_row, grad_pred_proj, (((0,), (0,)), ((), ())), preferred_element_type=jnp.float32
    )
    grad_bias_joint = jnp.sum(grad_pred_proj.astype(jnp.float32), axis=0)
    return (-log_total, (grad_enc, grad_pred, grad_out, grad_bias_out, grad_bias_joint))


def local_sums(enc, pred, labels, frame_len, label_len, w_enc, w_pred, b_joint, w_out, b_out):

    def forward_one(unused_carry, inputs):
        enc_row, pred_row, label_row = inputs
        return (
            None,
            joint_forward(enc_row, pred_row, label_row, w_enc, w_pred, b_joint, w_out, b_out),
        )

    unused_none, (hidden, log_probs, blank, emit) = lax.scan(forward_one, None, (enc, pred, labels))
    alpha, beta, below = lattice(blank, emit, frame_len, label_len)
    initial = (
        jnp.zeros(w_enc.shape, jnp.float32),
        jnp.zeros(w_pred.shape, jnp.float32),
        jnp.zeros(w_out.shape, jnp.float32),
        jnp.zeros(b_out.shape, jnp.float32),
        jnp.zeros(b_joint.shape, jnp.float32),
    )

    def backward_one(carry, inputs):
        loss_sum, grad_sums = carry
        loss_one, grads_one = joint_backward(*inputs, w_out)
        added = tuple((total + term for total, term in zip(grad_sums, grads_one)))
        return ((loss_sum + loss_one, added), None)

    (loss_sum, grads), unused_ys = lax.scan(
        backward_one,
        (jnp.float32(0.0), initial),
        (enc, pred, labels, hidden, log_probs, blank, emit, alpha, beta, below),
    )
    return (loss_sum, grads)


def squares(items):
    total_sq = jnp.float32(0.0)
    for item in items:
        total_sq = total_sq + jnp.sum(item * item)
    return total_sq


def per_device(enc, pred, labels, frame_len, label_len, w_enc, w_pred, b_joint, w_out, b_out):
    loss_local, grads = local_sums(
        enc, pred, labels, frame_len, label_len, w_enc, w_pred, b_joint, w_out, b_out
    )
    count_local = jnp.sum(label_len).astype(jnp.float32)
    param_count = jnp.float32(w_enc.size + w_pred.size + w_out.size + b_out.size + b_joint.size)
    loss_total, label_total = lax.psum((loss_local, count_local), ("dp", "rep"))
    summed = lax.psum((grads[0], grads[1], grads[2], grads[3], grads[4]), ("dp", "rep"))
    scale = lax.rsqrt(squares(summed) / param_count + EPS)
    result = tuple((item * scale for item in summed))
    return (result[0], result[1], result[2], result[3], result[4], loss_total / label_total)


def solution(mesh):
    in_specs = (
        P(("dp", "rep"), None, None),
        P(("dp", "rep"), None, None),
        P(("dp", "rep"), None),
        P(("dp", "rep")),
        P(("dp", "rep")),
        P(),
        P(),
        P(),
        P(),
        P(),
    )
    out_specs = (P(), P(), P(), P(), P(), P())
    return jax.shard_map(
        per_device, mesh=mesh, in_specs=in_specs, out_specs=out_specs, check_vma=False
    )
```

profile of v0, /device:TPU:0, one launch (start us, length us, event | category | flops | bytes accessed | tf_op | source)
XLA Modules:
  0.0 639.8 jit_solution(4801691328892887368)
XLA Ops:
  11.1 88.6 %while.58 = (s32[]{:T(128)}, bf16[2,816,640]{2,1,0:T(8,128)(2,1)}, f32[2,816,4096]{2,1,0:T(8,128)}, f32[2,48,17]{2,1,0:T(8,128)S(1)}, f32[2,48,17]{2,1,0:T(8,128...) while((s32[]{:T(128)}, bf16[2,816,640]{2,1,0:T(8,128)(2,1)}, ...), condition=%wide.region_4.5_spmd, body=%wide.region_0.4_spmd.sunk | while | flops 4369261056 | bytes 147507888 | solution.py:167
  16.4 7.5 %add_reduce_fusion.2 = (f32[816]{0:T(1024)S(1)}, f32[816,4096]{1,0:T(8,128)S(1)}) fusion(f32[4096]{0:T(1024)S(1)} %convert_element_type.65, bf16[816,640]{1,0:T(8,128)(2,1)S(1)} %convert_element_type.64, bf16[640,4096]{1,0:T(8,128)(2,1)} %get-tuple-element.1143), kind=kOutput, calls=%fused_computation.66.clone.1 | convolution fusion | flops 4284873984 | bytes 19676352 | tf_op jit(solution)/shard_map/while/body/eval_jaxpr/dot_general | solution.py:104
  26.2 2.5 copy-done.1
  28.9 12.7 %select_reduce_fusion.2 = (f32[816]{0:T(1024)S(1)}, f32[816,4096]{1,0:T(8,128)}) fusion(s32[816]{0:T(1024)S(1)} %eq.178, f32[816]{0:T(1024)S(1)} %log.11, f32[816]{0:T(1024)S(1)} %get-tuple-element.1053, f32[816,4096]{1,0:T(8,128)} %copy-done.1, f32[4096]{0:T(1024)S(1)} %convert_element_type.65), kind=kLoop, calls=%fused_computation.62.clone.1 | loop fusion | flops 20053200 | bytes 26768128 | tf_op jit(solution)/shard_map/while/body/eval_jaxpr/reduce_sum | solution.py:110
  43.1 11.3 %bitcast_dynamic-update-slice_fusion.5 = f32[2,816,4096]{2,1,0:T(8,128)} fusion(f32[2,816,4096]{2,1,0:T(8,128)} %get-tuple-element.1120, s32[]{:T(128)} %get-tuple-element.1118, f32[816,4096]{1,0:T(8,128)} %get-tuple-element.1054), kind=kLoop, calls=%fused_computation.61.clone.1 | loop fusion | bytes 26739200 | tf_op jit(solution)/shard_map/while/body/jit(dynamic_update_index_in_dim)/dynamic_update_slice | solution.py:167
  60.6 7.5 %add_reduce_fusion.2 = (f32[816]{0:T(1024)S(1)}, f32[816,4096]{1,0:T(8,128)S(1)}) fusion(f32[4096]{0:T(1024)S(1)} %convert_element_type.65, bf16[816,640]{1,0:T(8,128)(2,1)S(1)} %convert_element_type.64, bf16[640,4096]{1,0:T(8,128)(2,1)} %get-tuple-element.1143), kind=kOutput, calls=%fused_computation.66.clone.1 | convolution fusion | flops 4284873984 | bytes 19676352 | tf_op jit(solution)/shard_map/while/body/eval_jaxpr/dot_general | solution.py:104
  70.5 2.5 copy-done.1
  73.2 12.7 %select_reduce_fusion.2 = (f32[816]{0:T(1024)S(1)}, f32[816,4096]{1,0:T(8,128)}) fusion(s32[816]{0:T(1024)S(1)} %eq.178, f32[816]{0:T(1024)S(1)} %log.11, f32[816]{0:T(1024)S(1)} %get-tuple-element.1053, f32[816,4096]{1,0:T(8,128)} %copy-done.1, f32[4096]{0:T(1024)S(1)} %convert_element_type.65), kind=kLoop, calls=%fused_computation.62.clone.1 | loop fusion | flops 20053200 | bytes 26768128 | tf_op jit(solution)/shard_map/while/body/eval_jaxpr/reduce_sum | solution.py:110
  87.3 11.3 %bitcast_dynamic-update-slice_fusion.5 = f32[2,816,4096]{2,1,0:T(8,128)} fusion(f32[2,816,4096]{2,1,0:T(8,128)} %get-tuple-element.1120, s32[]{:T(128)} %get-tuple-element.1118, f32[816,4096]{1,0:T(8,128)} %get-tuple-element.1054), kind=kLoop, calls=%fused_computation.61.clone.1 | loop fusion | bytes 26739200 | tf_op jit(solution)/shard_map/while/body/jit(dynamic_update_index_in_dim)/dynamic_update_slice | solution.py:167
  100.8 12.3 %gather_fusion = f32[1088,2]{1,0:T(8,128)S(1)} fusion(f32[2,48,17]{0,1,2:T(8,128)S(1)} %copy.55, s32[1088]{0:T(1024)S(1)} %reshape.180), kind=kCustom, calls=%fused_computation | custom fusion | bytes 26112 | tf_op jit(solution)/shard_map/gather | solution.py:21
  113.6 12.1 %gather_fusion.1 = f32[1088,2]{1,0:T(8,128)S(1)} fusion(f32[2,48,17]{0,1,2:T(8,128)S(1)} %copy.57, s32[1088]{0:T(1024)S(1)} %reshape.180), kind=kCustom, calls=%fused_computation.1 | custom fusion | bytes 26112 | tf_op jit(solution)/shard_map/gather | solution.py:21
  126.3 106.5 %while.59 = (s32[]{:T(128)}, f32[2,17]{1,0:T(2,128)S(1)}, f32[2,17]{1,0:T(2,128)S(1)}, f32[64,2,17]{2,1,0:T(2,128)S(1)}, f32[64,2,17]{2,1,0:T(2,128)S(1)}, /*ind...) while((s32[]{:T(128)}, f32[2,17]{1,0:T(2,128)S(1)}, ...), condition=%wide.region_6.7_spmd.clone, body=%wide.region_5.6_spmd.clone.sunk | while | flops 1434 | bytes 22799 | solution.py:84
  233.9 9.8 %gather_fusion.2 = f32[816,2]{1,0:T(8,128)S(1)} fusion(f32[2,64,17]{0,1,2:T(8,128)S(1)} %bitcast.183, s32[816]{0:T(1024)S(1)} %reshape.192), kind=kCustom, calls=%fused_computation.2 | custom fusion | bytes 19584 | tf_op jit(solution)/shard_map/gather | solution.py:31
  245.2 10.0 %gather_fusion.4 = f32[816,2]{1,0:T(8,128)S(1)} fusion(f32[2,64,17]{0,1,2:T(8,128)S(1)} %bitcast.185, s32[816]{0:T(1024)S(1)} %reshape.192), kind=kCustom, calls=%fused_computation.4 | custom fusion | bytes 19584 | tf_op jit(solution)/shard_map/gather | solution.py:31
  256.3 9.8 %gather_fusion.3 = f32[816,2]{1,0:T(8,128)S(1)} fusion(f32[2,64,17]{0,1,2:T(8,128)S(1)} %bitcast.184, s32[816]{0:T(1024)S(1)} %reshape.192), kind=kCustom, calls=%fused_computation.3 | custom fusion | bytes 19584 | tf_op jit(solution)/shard_map/gather | solution.py:31
  266.5 91.0 %while.60 = (s32[]{:T(128)}, f32[]{:T(128)}, f32[640,640]{1,0:T(8,128)}, f32[640,640]{1,0:T(8,128)}, f32[640,4096]{1,0:T(8,128)}, /*index=5*/f32[4096]{0:T(1024)...) while((s32[]{:T(128)}, f32[]{:T(128)}, ...), condition=%wide.region_12.13_spmd.clone, body=%wide.region_7.12_spmd.clone.sunk | while | flops 8649718784 | bytes 146314000 | solution.py:183
  269.0 11.2 %fusion.89 = bf16[816,4096]{1,0:T(8,128)(2,1)} fusion(f32[2,816,4096]{2,1,0:T(8,128)} %get-tuple-element.1259, s32[]{:T(128)} %get-tuple-element.1229, f32[816]{0:T(1024)S(1)} %reshape.215, s32[816]{0:T(1024)S(1)} %eq.189, f32[816]{0:T(1024)S(1)} %exp.63, f32[816]{0:T(1024)S(1)} %add.404, pred[4096]{0:T(1024)(128)(4,1)S(1)} %iota_compare_fusion.4), kind=kLoop, calls=%fused_computation.33.clone.1 | loop fusion | flops 23396352 | bytes 20071172 | tf_op jit(solution)/shard_map/while/body/eval_jaxpr/convert_element_type | solution.py:134
  280.2 10.6 %select_add_fusion.12 = f32[640,4096]{1,0:T(8,128)} fusion(f32[640,4096]{1,0:T(8,128)} %get-tuple-element.1233, bf16[816,4096]{1,0:T(8,128)(2,1)} %fusion.89, pred[]{:T(512)S(6)} %compare.12, bf16[2,816,640]{2,1,0:T(8,128)(2,1)} %get-tuple-element.1266, s32[]{:T(128)} %get-tuple-element.1229), kind=kOutput, calls=%fused_computation.36.clone.1 | convolution fusion | flops 4283432960 | bytes 28701184 | tf_op jit(solution)/shard_map/while/body/eval_jaxpr/dot_general | solution.py:135
  290.8 8.1 %subtract_multiply_fusion.2 = f32[816,640]{1,0:T(8,128)} fusion(bf16[816,4096]{1,0:T(8,128)(2,1)S(1)} %copy-done, bf16[640,4096]{1,0:T(8,128)(2,1)S(1)} %bitcast.202, bf16[2,816,640]{2,1,0:T(8,128)(2,1)} %get-tuple-element.1266, s32[]{:T(128)} %get-tuple-element.1229), kind=kOutput, calls=%fused_computation.37.clone.1 | convolution fusion | flops 4280279040 | bytes 15060996 | tf_op jit(solution)/shard_map/while/body/eval_jaxpr/dot_general | solution.py:139
  299.0 3.1 reshape.216
  302.1 2.5 fusion.90
  312.2 11.2 %fusion.89 = bf16[816,4096]{1,0:T(8,128)(2,1)} fusion(f32[2,816,4096]{2,1,0:T(8,128)} %get-tuple-element.1259, s32[]{:T(128)} %get-tuple-element.1229, f32[816]{0:T(1024)S(1)} %reshape.215, s32[816]{0:T(1024)S(1)} %eq.189, f32[816]{0:T(1024)S(1)} %exp.63, f32[816]{0:T(1024)S(1)} %add.404, pred[4096]{0:T(1024)(128)(4,1)S(1)} %iota_compare_fusion.4), kind=kLoop, calls=%fused_computation.33.clone.1 | loop fusion | flops 23396352 | bytes 20071172 | tf_op jit(solution)/shard_map/while/body/eval_jaxpr/convert_element_type | solution.py:134
  323.4 12.1 %select_add_fusion.12 = f32[640,4096]{1,0:T(8,128)} fusion(f32[640,4096]{1,0:T(8,128)} %get-tuple-element.1233, bf16[816,4096]{1,0:T(8,128)(2,1)} %fusion.89, pred[]{:T(512)S(6)} %compare.12, bf16[2,816,640]{2,1,0:T(8,128)(2,1)} %get-tuple-element.1266, s32[]{:T(128)} %get-tuple-element.1229), kind=kOutput, calls=%fused_computation.36.clone.1 | convolution fusion | flops 4283432960 | bytes 28701184 | tf_op jit(solution)/shard_map/while/body/eval_jaxpr/dot_general | solution.py:135
  335.8 8.1 %subtract_multiply_fusion.2 = f32[816,640]{1,0:T(8,128)} fusion(bf16[816,4096]{1,0:T(8,128)(2,1)S(1)} %copy-done, bf16[640,4096]{1,0:T(8,128)(2,1)S(1)} %bitcast.202, bf16[2,816,640]{2,1,0:T(8,128)(2,1)} %get-tuple-element.1266, s32[]{:T(128)} %get-tuple-element.1229), kind=kOutput, calls=%fused_computation.37.clone.1 | convolution fusion | flops 4280279040 | bytes 15060996 | tf_op jit(solution)/shard_map/while/body/eval_jaxpr/dot_general | solution.py:139
  343.9 3.1 reshape.216
  347.0 2.5 fusion.90
  349.5 3.0 select_add_fusion.11
  352.6 3.0 select_add_fusion.10
  359.4 44.8 %all-reduce.5 = (f32[4096]{0:T(1024)S(1)}, f32[640]{0:T(1024)S(1)}, f32[]{:T(128)}, f32[]{:T(128)}) all-reduce(f32[4096]{0:T(1024)S(1)} %get-tuple-element.406, f32[640]{0:T(1024)S(1)} %get-tuple-element.407, f32[]{:T(128)} %get-tuple-element.408, f32[]{:T(128)S(6)} %convert_element_type.42), channel_id=1, replica_groups=mesh['dp'=8,'rep'=4] {'dp','rep'}, use_global_device_ids=true, to_apply=%region_19.20 | all-reduce | flops 4738 | bytes 37904 | tf_op jit(solution)/shard_map/psum | solution.py:205
  406.7 199.6 %all-reduce.9.cloned.1.call-done = (f32[640,640]{1,0:T(8,128)}, f32[640,640]{1,0:T(8,128)}, f32[640,4096]{1,0:T(8,128)}) async-done(((f32[640,640]{1,0:T(8,128)}, f32[640,640]{1,0:T(8,128)}, f32[640,4096]{1,0:T(8,128)}), (f32[640,640]{1,0:T(8,128)}, f32[640,640]{1,0:T(8,128)}, f32[640,4096]{1,0:T(8,128)})) %all-reduce.9.cloned.1.call-update) | async-done | bytes 13762576 | tf_op jit(solution)/shard_map/psum | solution.py:205
  606.3 7.4 %multiply_reduce_fusion = f32[]{:T(128)} fusion(f32[640,4096]{1,0:T(8,128)} %get-tuple-element.759), kind=kLoop, calls=%fused_computation.83 | loop fusion | flops 5242879 | bytes 10485764 | tf_op jit(solution)/shard_map/reduce_sum | solution.py:194
  619.2 9.7 %broadcast_multiply_fusion = f32[640,4096]{1,0:T(8,128)} fusion(f32[640,4096]{1,0:T(8,128)} %get-tuple-element.759, f32[]{:T(128)S(6)} %rsqrt.3), kind=kLoop, calls=%fused_computation.84 | loop fusion | flops 2621440 | bytes 20971524 | tf_op jit(solution)/shard_map/mul | solution.py:207
  (965 shorter events, 108.7 us)
Async XLA Ops:
  7.2 599.1 %all-reduce.9.cloned.1.call-start = ((), (), s32[]{:S(2)}) async-start(), calls=%async_computation | async-start | bytes 27525120 | tf_op jit(solution)/shard_map/psum | solution.py:205
  11.0 89.7 %copy-start.5 = (s32[64,17,1]{1,0,2:T(8,128)S(1)}, s32[64,17,1]{1,0,2:T(8,128)}, u32[]{:S(2)}) copy-start(s32[64,17,1]{1,0,2:T(8,128)} %fusion.34) | copy-start | bytes 13060
  11.0 115.0 %copy-start.14 = (pred[64,17]{1,0:T(8,128)(4,1)S(1)}, pred[64,17]{1,0:T(8,128)(4,1)}, u32[]{:S(2)}) copy-start(pred[64,17]{1,0:T(8,128)(4,1)} %compare_and_fusion) | copy-start | bytes 3268
  11.0 115.1 %copy-start.6 = (s32[64,17]{1,0:T(8,128)S(1)}, s32[64,17]{1,0:T(8,128)}, u32[]{:S(2)}) copy-start(s32[64,17]{1,0:T(8,128)} %iota_subtract_fusion) | copy-start | bytes 13060
  11.0 115.2 %copy-start.16 = (f32[17]{0:T(128)S(1)}, f32[17]{0:T(128)}, u32[]{:S(2)}) copy-start(f32[17]{0:T(128)} %compare_select_fusion.7) | copy-start | bytes 208
  11.1 115.2 %copy-start.7 = (s32[2]{0:T(128)S(1)}, s32[2]{0:T(128)}, u32[]{:S(2)}) copy-start(s32[2]{0:T(128)} %param.20) | copy-start | bytes 28
  11.1 115.2 %copy-start.10 = (f32[64,2,17]{2,1,0:T(2,128)S(1)}, f32[64,2,17]{2,1,0:T(2,128)}, u32[]{:S(2)}) copy-start(f32[64,2,17]{2,1,0:T(2,128)} %custom-call.20) | copy-start | bytes 26116
  11.1 115.2 %copy-start.11 = (f32[64,2,17]{2,1,0:T(2,128)S(1)}, f32[64,2,17]{2,1,0:T(2,128)}, u32[]{:S(2)}) copy-start(f32[64,2,17]{2,1,0:T(2,128)} %custom-call.21) | copy-start | bytes 26116
  11.1 115.2 %copy-start.12 = (f32[64,2,17]{2,1,0:T(2,128)S(1)}, f32[64,2,17]{2,1,0:T(2,128)}, u32[]{:S(2)}) copy-start(f32[64,2,17]{2,1,0:T(2,128)} %custom-call.22) | copy-start | bytes 26116
  11.1 115.2 %copy-start.13 = (s32[2]{0:T(128)S(1)}, s32[2]{0:T(128)}, u32[]{:S(2)}) copy-start(s32[2]{0:T(128)} %param.19) | copy-start | bytes 28
  11.1 115.2 %copy-start.15 = (f32[2,17]{1,0:T(2,128)S(1)}, f32[2,17]{1,0:T(2,128)}, u32[]{:S(2)}) copy-start(f32[2,17]{1,0:T(2,128)} %custom-call.10) | copy-start | bytes 412
  23.9 4.8 copy-start.1
  23.9 4.8 copy-start.17
  68.1 4.8 copy-start.1
  68.1 4.8 copy-start.17
  99.7 134.1 %copy-start.9 = (s32[48,17,1]{1,0,2:T(8,128)S(1)}, s32[48,17,1]{1,0,2:T(8,128)}, u32[]{:S(2)}) copy-start(s32[48,17,1]{1,0,2:T(8,128)} %fusion.37) | copy-start | bytes 9796
  113.2 153.3 %copy-start.4 = (bf16[2,48,640]{2,1,0:T(8,128)(2,1)S(1)}, bf16[2,48,640]{2,1,0:T(8,128)(2,1)}, u32[]{:S(2)}) copy-start(bf16[2,48,640]{2,1,0:T(8,128)(2,1)} %get-tuple-element.1284) | copy-start | bytes 368644
  113.2 153.3 %copy-start.18 = (s32[2,16]{1,0:T(2,128)S(1)}, s32[2,16]{1,0:T(2,128)}, u32[]{:S(2)}) copy-start(s32[2,16]{1,0:T(2,128)} %get-tuple-element.1288) | copy-start | bytes 388
  269.0 21.8 %slice-start.2 = ((s8[5242880]{0:T(1024)(128)(4,1)}), s8[1048576]{0:T(1024)(128)(4,1)S(1)}, s32[]{:S(2)}) async-start(s8[5242880]{0:T(1024)(128)(4,1)} %bitcast.201), calls=%async_computation.3 | async-start | bytes 2097152 | tf_op jit(solution)/shard_map/while
  280.2 10.6 %copy-start = (bf16[816,4096]{1,0:T(8,128)(2,1)S(1)}, bf16[816,4096]{1,0:T(8,128)(2,1)}, u32[]{:S(2)}) copy-start(bf16[816,4096]{1,0:T(8,128)(2,1)} %fusion.89) | copy-start | bytes 20054020 | tf_op jit(solution)/shard_map/while
  280.2 10.6 %slice-start.3 = ((s8[5242880]{0:T(1024)(128)(4,1)}), s8[4194304]{0:T(1024)(128)(4,1)S(1)}, s32[]{:S(2)}) async-start(s8[5242880]{0:T(1024)(128)(4,1)} %bitcast.201), calls=%async_computation.4 | async-start | bytes 8388608 | tf_op jit(solution)/shard_map/while
  299.0 8.8 %slice-start = ((s8[6684672]{0:T(1024)(128)(4,1)}), s8[2490368]{0:T(1024)(128)(4,1)S(1)}, s32[]{:S(2)}) async-start(s8[6684672]{0:T(1024)(128)(4,1)} %bitcast.181), calls=%async_computation.1 | async-start | bytes 4980736 | tf_op jit(solution)/shard_map/while
  302.1 5.7 slice-start.1
  312.2 23.3 %slice-start.2 = ((s8[5242880]{0:T(1024)(128)(4,1)}), s8[1048576]{0:T(1024)(128)(4,1)S(1)}, s32[]{:S(2)}) async-start(s8[5242880]{0:T(1024)(128)(4,1)} %bitcast.201), calls=%async_computation.3 | async-start | bytes 2097152 | tf_op jit(solution)/shard_map/while
  323.4 12.1 %copy-start = (bf16[816,4096]{1,0:T(8,128)(2,1)S(1)}, bf16[816,4096]{1,0:T(8,128)(2,1)}, u32[]{:S(2)}) copy-start(bf16[816,4096]{1,0:T(8,128)(2,1)} %fusion.89) | copy-start | bytes 20054020 | tf_op jit(solution)/shard_map/while
  323.4 12.4 %slice-start.3 = ((s8[5242880]{0:T(1024)(128)(4,1)}), s8[4194304]{0:T(1024)(128)(4,1)S(1)}, s32[]{:S(2)}) async-start(s8[5242880]{0:T(1024)(128)(4,1)} %bitcast.201), calls=%async_computation.4 | async-start | bytes 8388608 | tf_op jit(solution)/shard_map/while
  343.9 11.7 %slice-start = ((s8[6684672]{0:T(1024)(128)(4,1)}), s8[2490368]{0:T(1024)(128)(4,1)S(1)}, s32[]{:S(2)}) async-start(s8[6684672]{0:T(1024)(128)(4,1)} %bitcast.181), calls=%async_computation.1 | async-start | bytes 4980736 | tf_op jit(solution)/shard_map/while
  347.0 8.6 %slice-start.1 = ((s8[6684672]{0:T(1024)(128)(4,1)}), s8[4194304]{0:T(1024)(128)(4,1)S(1)}, s32[]{:S(2)}) async-start(s8[6684672]{0:T(1024)(128)(4,1)} %bitcast.181), calls=%async_computation.2 | async-start | bytes 8388608 | tf_op jit(solution)/shard_map/while
  357.4 0.7 copy-start.8
  606.3 7.4 %copy-start.2 = (f32[640,640]{1,0:T(8,128)S(1)}, f32[640,640]{1,0:T(8,128)}, u32[]{:S(2)}) copy-start(f32[640,640]{1,0:T(8,128)} %get-tuple-element.757) | copy-start | bytes 4915204
  606.3 7.4 %copy-start.3 = (f32[640,640]{1,0:T(8,128)S(1)}, f32[640,640]{1,0:T(8,128)}, u32[]{:S(2)}) copy-start(f32[640,640]{1,0:T(8,128)} %get-tuple-element.758) | copy-start | bytes 4915204
Sparse Core Ops, SparseCore 0:
  357.6 248.6 all-reduce.8
where the time goes:
time: 649 us; the launch traced here: 640 us
  waiting for transfers between devices  200 us (31%)
  local copies, waits for them, and re-layouts  149 us (23%)
  other arithmetic  109 us (17%)
  matrix products  68.8 us (11%)
  loops' own time  47.9 us (7%)
  blocking collectives  44.8 us (7%)
  between operations  21.2 us (3%)
    psum x1, waiting for transfers between devices, per_device(): lax.psum((grads[0], grads[1], grads[2], grads[3], grads[4]), ('dp', 'rep'))  200 us
    another operation x1, loops' own time, lattice(): lax.scan(both_ways, (first_diag, neg_grid), inputs)  46.1 us
    psum x1, blocking collectives, per_device(): lax.psum((grads[0], grads[1], grads[2], grads[3], grads[4]), ('dp', 'rep'))  44.8 us
    dynamic_slice x256, local copies, waits for them, and re-layouts, lattice(): lax.scan(both_ways, (first_diag, neg_grid), inputs)  39.8 us
    gather x9, local copies, waits for them, and re-layouts, unskewed(): by_utterance[:, frame_ids[:, None] + positions[None, :], positions[None, :]]  30.5 us
    reduce_sum x2, other arithmetic, joint_forward(): jnp.sum(jnp.where(is_target, log_probs, 0.0), axis=1)  25.4 us
    gather x6, local copies, waits for them, and re-layouts, skewed(): grid[:, jnp.clip(frame_index, 0, num_frames - 1), positions[None, :]]  25.2 us
    dynamic_update_slice x6, local copies, waits for them, and re-layouts, local_sums(): lax.scan(forward_one, None, (enc, pred, labels))  24.7 us
  transfers between devices with their start and end apart: 1, of which 1 were waited for; matrix products, arithmetic and copies ran while one was open for 0% of the time, Pallas kernels for 0%

commit v1 on v0

--- a/solution.py
+++ b/solution.py
@@ -202,7 +202,7 @@
     count_local = jnp.sum(label_len).astype(jnp.float32)
     param_count = jnp.float32(w_enc.size + w_pred.size + w_out.size + b_out.size + b_joint.size)
     loss_total, label_total = lax.psum((loss_local, count_local), ("dp", "rep"))
-    summed = lax.psum((grads[0], grads[1], grads[2], grads[3], grads[4]), ("dp", "rep"))
+    summed = lax.psum(lax.psum((grads[0], grads[1], grads[2], grads[3], grads[4]), "dp"), "rep")
     scale = lax.rsqrt(squares(summed) / param_count + EPS)
     result = tuple((item * scale for item in summed))
     return (result[0], result[1], result[2], result[3], result[4], loss_total / label_total)

time: 649 us -> 1070 us (1.65)
  waiting for transfers between devices: 200 us -> 578 us
  blocking collectives: 44.8 us -> 90.4 us
    psum x1 -> x2, waiting for transfers between devices: 200 us -> 578 us  [the longest x1 430 us: per_device(): lax.psum((grads[0], grads[1], grads[2], grads[3], grads[4]), 'dp')]
    psum x1 -> x3, blocking collectives: 44.8 us -> 90.4 us  [the longest x1 41.2 us: per_device(): loss_total, label_total = lax.psum((loss_local, count_local), ('dp', 'rep'))]
  transfers between devices with their start and end apart: 1 -> 2, of which waited for: 1 -> 2; matrix products, arithmetic and copies ran while one was open for 0% -> 0% of each run, Pallas kernels for 0% -> 0%
where the time goes in v1:
time: 1070 us; the launch traced here: 1060 us
  waiting for transfers between devices  578 us (54%)
  local copies, waits for them, and re-layouts  149 us (14%)
  other arithmetic  109 us (10%)
  blocking collectives  90.4 us (8%)
  matrix products  68.8 us (6%)
  loops' own time  48.1 us (4%)
  between operations  21.3 us (2%)
    psum x1, waiting for transfers between devices, per_device(): lax.psum((grads[0], grads[1], grads[2], grads[3], grads[4]), 'dp')  430 us
    psum x1, waiting for transfers between devices, per_device(): lax.psum(lax.psum((grads[0], grads[1], grads[2], grads[3], grads[4]), 'dp...  148 us
    another operation x1, loops' own time, lattice(): lax.scan(both_ways, (first_diag, neg_grid), inputs)  46.1 us
    psum x1, blocking collectives, per_device(): loss_total, label_total = lax.psum((loss_local, count_local), ('dp', 'rep'))  41.2 us
    dynamic_slice x256, local copies, waits for them, and re-layouts, lattice(): lax.scan(both_ways, (first_diag, neg_grid), inputs)  39.8 us
    psum x1, blocking collectives, per_device(): lax.psum((grads[0], grads[1], grads[2], grads[3], grads[4]), 'dp')  37 us
    gather x9, local copies, waits for them, and re-layouts, unskewed(): by_utterance[:, frame_ids[:, None] + positions[None, :], positions[None, :]]  30.3 us
    reduce_sum x2, other arithmetic, joint_forward(): jnp.sum(jnp.where(is_target, log_probs, 0.0), axis=1)  25.4 us
  transfers between devices with their start and end apart: 2, of which 2 were waited for; matrix products, arithmetic and copies ran while one was open for 0% of the time, Pallas kernels for 0%

profile of v1, /device:TPU:0, one launch (start us, length us, event | category | flops | bytes accessed | tf_op | source)
XLA Modules:
  0.0 1064.1 jit_solution(16192252922041012584)
XLA Ops:
  11.1 88.6 %while.58 = (s32[]{:T(128)}, bf16[2,816,640]{2,1,0:T(8,128)(2,1)}, f32[2,816,4096]{2,1,0:T(8,128)}, f32[2,48,17]{2,1,0:T(8,128)S(1)}, f32[2,48,17]{2,1,0:T(8,128...) while((s32[]{:T(128)}, bf16[2,816,640]{2,1,0:T(8,128)(2,1)}, ...), condition=%wide.region_4.5_spmd, body=%wide.region_0.4_spmd.sunk | while | flops 4369261056 | bytes 147507888 | solution.py:167
  16.4 7.5 add_reduce_fusion.2
  28.9 12.7 %select_reduce_fusion.2 = (f32[816]{0:T(1024)S(1)}, f32[816,4096]{1,0:T(8,128)}) fusion(s32[816]{0:T(1024)S(1)} %eq.178, f32[816]{0:T(1024)S(1)} %log.11, f32[816]{0:T(1024)S(1)} %get-tuple-element.1058, f32[816,4096]{1,0:T(8,128)} %copy-done.1, f32[4096]{0:T(1024)S(1)} %convert_element_type.65), kind=kLoop, calls=%fused_computation.62.clone.1 | loop fusion | flops 20053200 | bytes 26768128 | tf_op jit(solution)/shard_map/while/body/eval_jaxpr/reduce_sum | solution.py:110
  43.1 11.3 %bitcast_dynamic-update-slice_fusion.5 = f32[2,816,4096]{2,1,0:T(8,128)} fusion(f32[2,816,4096]{2,1,0:T(8,128)} %get-tuple-element.1125, s32[]{:T(128)} %get-tuple-element.1123, f32[816,4096]{1,0:T(8,128)} %get-tuple-element.1059), kind=kLoop, calls=%fused_computation.61.clone.1 | loop fusion | bytes 26739200 | tf_op jit(solution)/shard_map/while/body/jit(dynamic_update_index_in_dim)/dynamic_update_slice | solution.py:167
  60.6 7.5 add_reduce_fusion.2
  73.2 12.7 %select_reduce_fusion.2 = (f32[816]{0:T(1024)S(1)}, f32[816,4096]{1,0:T(8,128)}) fusion(s32[816]{0:T(1024)S(1)} %eq.178, f32[816]{0:T(1024)S(1)} %log.11, f32[816]{0:T(1024)S(1)} %get-tuple-element.1058, f32[816,4096]{1,0:T(8,128)} %copy-done.1, f32[4096]{0:T(1024)S(1)} %convert_element_type.65), kind=kLoop, calls=%fused_computation.62.clone.1 | loop fusion | flops 20053200 | bytes 26768128 | tf_op jit(solution)/shard_map/while/body/eval_jaxpr/reduce_sum | solution.py:110
  87.3 11.3 %bitcast_dynamic-update-slice_fusion.5 = f32[2,816,4096]{2,1,0:T(8,128)} fusion(f32[2,816,4096]{2,1,0:T(8,128)} %get-tuple-element.1125, s32[]{:T(128)} %get-tuple-element.1123, f32[816,4096]{1,0:T(8,128)} %get-tuple-element.1059), kind=kLoop, calls=%fused_computation.61.clone.1 | loop fusion | bytes 26739200 | tf_op jit(solution)/shard_map/while/body/jit(dynamic_update_index_in_dim)/dynamic_update_slice | solution.py:167
  100.8 12.3 %gather_fusion = f32[1088,2]{1,0:T(8,128)S(1)} fusion(f32[2,48,17]{0,1,2:T(8,128)S(1)} %copy.55, s32[1088]{0:T(1024)S(1)} %reshape.180), kind=kCustom, calls=%fused_computation | custom fusion | bytes 26112 | tf_op jit(solution)/shard_map/gather | solution.py:21
  113.6 12.1 %gather_fusion.1 = f32[1088,2]{1,0:T(8,128)S(1)} fusion(f32[2,48,17]{0,1,2:T(8,128)S(1)} %copy.57, s32[1088]{0:T(1024)S(1)} %reshape.180), kind=kCustom, calls=%fused_computation.1 | custom fusion | bytes 26112 | tf_op jit(solution)/shard_map/gather | solution.py:21
  126.3 106.5 %while.59 = (s32[]{:T(128)}, f32[2,17]{1,0:T(2,128)S(1)}, f32[2,17]{1,0:T(2,128)S(1)}, f32[64,2,17]{2,1,0:T(2,128)S(1)}, f32[64,2,17]{2,1,0:T(2,128)S(1)}, /*ind...) while((s32[]{:T(128)}, f32[2,17]{1,0:T(2,128)S(1)}, ...), condition=%wide.region_6.7_spmd.clone, body=%wide.region_5.6_spmd.clone.sunk | while | flops 1434 | bytes 22799 | solution.py:84
  233.9 9.8 gather_fusion.2
  245.2 9.8 gather_fusion.4
  256.0 9.8 gather_fusion.3
  266.2 91.1 %while.60 = (s32[]{:T(128)}, f32[]{:T(128)}, f32[640,640]{1,0:T(8,128)}, f32[640,640]{1,0:T(8,128)}, f32[640,4096]{1,0:T(8,128)}, /*index=5*/f32[4096]{0:T(1024)...) while((s32[]{:T(128)}, f32[]{:T(128)}, ...), condition=%wide.region_12.13_spmd.clone, body=%wide.region_7.12_spmd.clone.sunk | while | flops 8649718784 | bytes 146314000 | solution.py:183
  269.0 11.2 %fusion.89 = bf16[816,4096]{1,0:T(8,128)(2,1)} fusion(f32[2,816,4096]{2,1,0:T(8,128)} %get-tuple-element.1264, s32[]{:T(128)} %get-tuple-element.1234, f32[816]{0:T(1024)S(1)} %reshape.215, s32[816]{0:T(1024)S(1)} %eq.189, f32[816]{0:T(1024)S(1)} %exp.63, f32[816]{0:T(1024)S(1)} %add.414, pred[4096]{0:T(1024)(128)(4,1)S(1)} %iota_compare_fusion.4), kind=kLoop, calls=%fused_computation.33.clone.1 | loop fusion | flops 23396352 | bytes 20071172 | tf_op jit(solution)/shard_map/while/body/eval_jaxpr/convert_element_type | solution.py:134
  280.2 10.6 select_add_fusion.12
  290.8 8.1 subtract_multiply_fusion.2
  299.0 3.1 reshape.216
  302.1 2.5 fusion.90
  312.2 11.2 %fusion.89 = bf16[816,4096]{1,0:T(8,128)(2,1)} fusion(f32[2,816,4096]{2,1,0:T(8,128)} %get-tuple-element.1264, s32[]{:T(128)} %get-tuple-element.1234, f32[816]{0:T(1024)S(1)} %reshape.215, s32[816]{0:T(1024)S(1)} %eq.189, f32[816]{0:T(1024)S(1)} %exp.63, f32[816]{0:T(1024)S(1)} %add.414, pred[4096]{0:T(1024)(128)(4,1)S(1)} %iota_compare_fusion.4), kind=kLoop, calls=%fused_computation.33.clone.1 | loop fusion | flops 23396352 | bytes 20071172 | tf_op jit(solution)/shard_map/while/body/eval_jaxpr/convert_element_type | solution.py:134
  323.4 12.1 %select_add_fusion.12 = f32[640,4096]{1,0:T(8,128)} fusion(f32[640,4096]{1,0:T(8,128)} %get-tuple-element.1238, bf16[816,4096]{1,0:T(8,128)(2,1)} %fusion.89, pred[]{:T(512)S(6)} %compare.12, bf16[2,816,640]{2,1,0:T(8,128)(2,1)} %get-tuple-element.1271, s32[]{:T(128)} %get-tuple-element.1234), kind=kOutput, calls=%fused_computation.36.clone.1 | convolution fusion | flops 4283432960 | bytes 28701184 | tf_op jit(solution)/shard_map/while/body/eval_jaxpr/dot_general | solution.py:135
  335.8 8.1 subtract_multiply_fusion.2
  343.9 3.1 reshape.216
  349.5 3.0 select_add_fusion.11
  352.5 3.0 select_add_fusion.10
  357.5 429.8 %all-reduce.13.cloned.1.call-done = (f32[640,640]{1,0:T(8,128)}, f32[640,640]{1,0:T(8,128)}, f32[640,4096]{1,0:T(8,128)}) async-done(((f32[640,640]{1,0:T(8,128)}, f32[640,640]{1,0:T(8,128)}, f32[640,4096]{1,0:T(8,128)}), (f32[640,640]{1,0:T(8,128)}, f32[640,640]{1,0:T(8,128)}, f32[640,4096]{1,0:T(8,128)})) %all-reduce.13.cloned.1.call-update) | async-done | bytes 13762576 | tf_op jit(solution)/shard_map/psum | solution.py:205
  789.3 41.2 %all-reduce.5 = (f32[]{:T(128)}, f32[]{:T(128)}) all-reduce(f32[]{:T(128)} %get-tuple-element.408, f32[]{:T(128)S(6)} %convert_element_type.42), channel_id=1, replica_groups=mesh['dp'=8,'rep'=4] {'dp','rep'}, use_global_device_ids=true, to_apply=%region_28.29 | all-reduce | flops 2 | bytes 16 | tf_op jit(solution)/shard_map/psum | solution.py:204
  831.8 37.0 %all-reduce.6 = (f32[4096]{0:T(1024)S(1)}, f32[640]{0:T(1024)S(1)}) all-reduce(f32[4096]{0:T(1024)S(1)} %get-tuple-element.406, f32[640]{0:T(1024)S(1)} %get-tuple-element.407), channel_id=1, replica_groups=mesh['dp'=8,'rep'=4] {'dp'}, use_global_device_ids=true, to_apply=%region_22.23 | all-reduce | flops 4736 | bytes 37888 | tf_op jit(solution)/shard_map/psum | solution.py:205
  868.8 12.2 %all-reduce.8 = (f32[4096]{0:T(1024)S(1)}, f32[640]{0:T(1024)S(1)}) all-reduce(f32[4096]{0:T(1024)S(1)} %get-tuple-element.755, f32[640]{0:T(1024)S(1)} %get-tuple-element.756), channel_id=1, replica_groups=mesh['dp'=8,'rep'=4] {'rep'}, use_global_device_ids=true, to_apply=%region_23.24 | all-reduce | flops 4736 | bytes 37888 | tf_op jit(solution)/shard_map/psum | solution.py:205
  882.2 148.4 %all-reduce.15.cloned.1.call-done = (f32[640,640]{1,0:T(8,128)}, f32[640,640]{1,0:T(8,128)}, f32[640,4096]{1,0:T(8,128)}) async-done(((f32[640,640]{1,0:T(8,128)}, f32[640,640]{1,0:T(8,128)}, f32[640,4096]{1,0:T(8,128)}), (f32[640,640]{1,0:T(8,128)}, f32[640,640]{1,0:T(8,128)}, f32[640,4096]{1,0:T(8,128)})) %all-reduce.15.cloned.1.call-update) | async-done | bytes 13762576 | tf_op jit(solution)/shard_map/psum | solution.py:205
  1030.6 7.4 multiply_reduce_fusion
  1043.5 9.7 broadcast_multiply_fusion
  (970 shorter events, 116.2 us)
Async XLA Ops:
  7.2 780.1 %all-reduce.13.cloned.1.call-start = ((), (), s32[]{:S(2)}) async-start(), calls=%async_computation | async-start | bytes 27525120 | tf_op jit(solution)/shard_map/psum | solution.py:205
  11.0 89.7 %copy-start.5 = (s32[64,17,1]{1,0,2:T(8,128)S(1)}, s32[64,17,1]{1,0,2:T(8,128)}, u32[]{:S(2)}) copy-start(s32[64,17,1]{1,0,2:T(8,128)} %fusion.34) | copy-start | bytes 13060
  11.0 115.0 %copy-start.14 = (pred[64,17]{1,0:T(8,128)(4,1)S(1)}, pred[64,17]{1,0:T(8,128)(4,1)}, u32[]{:S(2)}) copy-start(pred[64,17]{1,0:T(8,128)(4,1)} %compare_and_fusion) | copy-start | bytes 3268
  11.0 115.1 %copy-start.6 = (s32[64,17]{1,0:T(8,128)S(1)}, s32[64,17]{1,0:T(8,128)}, u32[]{:S(2)}) copy-start(s32[64,17]{1,0:T(8,128)} %iota_subtract_fusion) | copy-start | bytes 13060
  11.0 115.2 %copy-start.16 = (f32[17]{0:T(128)S(1)}, f32[17]{0:T(128)}, u32[]{:S(2)}) copy-start(f32[17]{0:T(128)} %compare_select_fusion.7) | copy-start | bytes 208
  11.1 115.2 %copy-start.7 = (s32[2]{0:T(128)S(1)}, s32[2]{0:T(128)}, u32[]{:S(2)}) copy-start(s32[2]{0:T(128)} %param.20) | copy-start | bytes 28
  11.1 115.2 %copy-start.10 = (f32[64,2,17]{2,1,0:T(2,128)S(1)}, f32[64,2,17]{2,1,0:T(2,128)}, u32[]{:S(2)}) copy-start(f32[64,2,17]{2,1,0:T(2,128)} %custom-call.20) | copy-start | bytes 26116
  11.1 115.2 %copy-start.11 = (f32[64,2,17]{2,1,0:T(2,128)S(1)}, f32[64,2,17]{2,1,0:T(2,128)}, u32[]{:S(2)}) copy-start(f32[64,2,17]{2,1,0:T(2,128)} %custom-call.21) | copy-start | bytes 26116
  11.1 115.2 %copy-start.12 = (f32[64,2,17]{2,1,0:T(2,128)S(1)}, f32[64,2,17]{2,1,0:T(2,128)}, u32[]{:S(2)}) copy-start(f32[64,2,17]{2,1,0:T(2,128)} %custom-call.22) | copy-start | bytes 26116
  11.1 115.2 %copy-start.13 = (s32[2]{0:T(128)S(1)}, s32[2]{0:T(128)}, u32[]{:S(2)}) copy-start(s32[2]{0:T(128)} %param.19) | copy-start | bytes 28
  11.1 115.2 %copy-start.15 = (f32[2,17]{1,0:T(2,128)S(1)}, f32[2,17]{1,0:T(2,128)}, u32[]{:S(2)}) copy-start(f32[2,17]{1,0:T(2,128)} %custom-call.10) | copy-start | bytes 412
  23.9 4.8 copy-start.1
  23.9 4.8 copy-start.17
  68.1 4.8 copy-start.1
  68.1 4.8 copy-start.17
  99.7 134.1 %copy-start.9 = (s32[48,17,1]{1,0,2:T(8,128)S(1)}, s32[48,17,1]{1,0,2:T(8,128)}, u32[]{:S(2)}) copy-start(s32[48,17,1]{1,0,2:T(8,128)} %fusion.37) | copy-start | bytes 9796
  113.2 153.1 %copy-start.4 = (bf16[2,48,640]{2,1,0:T(8,128)(2,1)S(1)}, bf16[2,48,640]{2,1,0:T(8,128)(2,1)}, u32[]{:S(2)}) copy-start(bf16[2,48,640]{2,1,0:T(8,128)(2,1)} %get-tuple-element.1299) | copy-start | bytes 368644
  113.2 153.1 %copy-start.18 = (s32[2,16]{1,0:T(2,128)S(1)}, s32[2,16]{1,0:T(2,128)}, u32[]{:S(2)}) copy-start(s32[2,16]{1,0:T(2,128)} %get-tuple-element.1307) | copy-start | bytes 388
  269.0 21.8 %slice-start.2 = ((s8[5242880]{0:T(1024)(128)(4,1)}), s8[1048576]{0:T(1024)(128)(4,1)S(1)}, s32[]{:S(2)}) async-start(s8[5242880]{0:T(1024)(128)(4,1)} %bitcast.201), calls=%async_computation.4 | async-start | bytes 2097152 | tf_op jit(solution)/shard_map/while
  280.2 10.6 copy-start
  280.2 10.6 slice-start.3
  299.0 8.8 slice-start
  302.1 5.7 slice-start.1
  312.2 23.3 %slice-start.2 = ((s8[5242880]{0:T(1024)(128)(4,1)}), s8[1048576]{0:T(1024)(128)(4,1)S(1)}, s32[]{:S(2)}) async-start(s8[5242880]{0:T(1024)(128)(4,1)} %bitcast.201), calls=%async_computation.4 | async-start | bytes 2097152 | tf_op jit(solution)/shard_map/while
  323.4 12.1 %copy-start = (bf16[816,4096]{1,0:T(8,128)(2,1)S(1)}, bf16[816,4096]{1,0:T(8,128)(2,1)}, u32[]{:S(2)}) copy-start(bf16[816,4096]{1,0:T(8,128)(2,1)} %fusion.89) | copy-start | bytes 20054020 | tf_op jit(solution)/shard_map/while
  323.4 12.4 %slice-start.3 = ((s8[5242880]{0:T(1024)(128)(4,1)}), s8[4194304]{0:T(1024)(128)(4,1)S(1)}, s32[]{:S(2)}) async-start(s8[5242880]{0:T(1024)(128)(4,1)} %bitcast.201), calls=%async_computation.5 | async-start | bytes 8388608 | tf_op jit(solution)/shard_map/while
  343.9 11.7 %slice-start = ((s8[6684672]{0:T(1024)(128)(4,1)}), s8[2490368]{0:T(1024)(128)(4,1)S(1)}, s32[]{:S(2)}) async-start(s8[6684672]{0:T(1024)(128)(4,1)} %bitcast.181), calls=%async_computation.2 | async-start | bytes 4980736 | tf_op jit(solution)/shard_map/while
  347.0 8.6 slice-start.1
  357.4 673.1 %all-reduce.15.cloned.1.call-start = ((), (), s32[]{:S(2)}) async-start(), calls=%async_computation.1 | async-start | bytes 27525120 | tf_op jit(solution)/shard_map/psum | solution.py:205
  787.3 0.7 copy-start.8
  1030.6 7.4 copy-start.2
  1030.6 7.4 copy-start.3
Sparse Core Ops, SparseCore 0:
  357.5 429.7 all-reduce.12
  790.0 240.4 all-reduce.14
